TPU v7x, 256 devices: a whole 4x4x8 slice. The times are simulated.
256 devices in a mesh: ens: 2 (over z_lo), ctx: 16 (over y, x), group: 8 (over z_hi, core).
Axes of the slice: x: 4, y: 4, z: 8 (z_hi: 4, z_lo: 2; z = z_hi * 2 + z_lo), core: 2. Of those that a mesh axis runs over, the one named last changes fastest.
Arguments:
- latents: bfloat16 [32, 4096, 512], P('ens', ('ctx', 'group')), parts along dimension 0, may hold values from -6 to 6
- rotary_rows: bfloat16 [32, 4096, 64], P('ens', ('ctx', 'group')), parts along dimension 0, may hold values from -6 to 6
- latent_gain: float32 [512], replicated, may hold values from 0.25 to 1.75
- key_up: bfloat16 [1024, 16, 128], P('ens', 'group'), parts along dimension 0, may hold values from -0.25 to 0.25
- value_up: bfloat16 [1024, 16, 128], P('ens', 'group'), parts along dimension 0, may hold values from -0.25 to 0.25
Outputs:
- stored_keys: bfloat16 [32, 16, 192, 4096], P(('ens', 'ctx'), 'group'), parts along dimension 0
- stored_values: bfloat16 [32, 4096, 16, 128], P(('ens', 'ctx'), None, 'group'), parts along dimension 0
There are 2 independent parts, one for each index of `ens`. A program takes and returns all parts, laid end to end along the dimension named above; an argument that names none is the same for every part. Nothing has to cross between parts.
All inputs are finite; a program needn't handle non-finite values.
Results may differ from a plain program's by a relative error of at most 0.0049.
Values may be sent and summed in bfloat16 or wider, within the bound.
A program may use at most 64 MiB of HBM per device.

v0:
```python
import jax
import jax.numpy as jnp
from jax import lax
from jax.sharding import PartitionSpec as P


def in_one_piece(arrays, axis, split_dim, concat_dim, along):
    ends, at = ([], 0)
    for a in arrays[:-1]:
        at += a.shape[along]
        ends.append(at)
    both = jnp.concatenate(arrays, axis=along)
    return tuple(
        jnp.split(
            lax.all_to_all(both, axis, split_axis=split_dim, concat_axis=concat_dim, tiled=True),
            ends,
            axis=along,
        )
    )


def to_heads(rows, rotary, key_up, value_up):
    wide_keys = jnp.einsum(
        "btr,rhk->bthk", rows, key_up, preferred_element_type=jnp.float32
    ).astype(jnp.bfloat16)
    shared = jnp.broadcast_to(rotary[:, :, None], wide_keys.shape[:3] + rotary.shape[2:])
    wide_values = jnp.einsum(
        "btr,rhk->bthk", rows, value_up, preferred_element_type=jnp.float32
    ).astype(jnp.bfloat16)
    return (jnp.concatenate([wide_keys, shared], axis=-1), wide_values)


def root_norm(vectors, row_gain):
    return (
        vectors * lax.rsqrt(jnp.mean(vectors * vectors, axis=-1, keepdims=True) + 1e-06) * row_gain
    )


def per_device(latents, rotary_rows, latent_gain, key_up, value_up):
    rows_ready = root_norm(latents.astype(jnp.float32), latent_gain).astype(jnp.bfloat16)
    rows_moved, rotary_moved = in_one_piece((rows_ready, rotary_rows), "ctx", 0, 1, 2)
    rows_cut = rows_moved.reshape(
        rows_moved.shape[0], lax.axis_size("ctx"), -1, rows_moved.shape[2]
    )
    rotary_cut = rotary_moved.reshape(
        rotary_moved.shape[0], lax.axis_size("ctx"), -1, rotary_moved.shape[2]
    )
    rows_joined, rotary_joined = (
        lax.all_gather(rows_cut, "group", axis=2, tiled=True),
        lax.all_gather(rotary_cut, "group", axis=2, tiled=True),
    )
    rows_whole = rows_joined.reshape(rows_joined.shape[0], -1, rows_joined.shape[3])
    rotary_whole = rotary_joined.reshape(rotary_joined.shape[0], -1, rotary_joined.shape[3])
    stored_keys, stored_values = to_heads(rows_whole, rotary_whole, key_up, value_up)
    stored_keys = jnp.transpose(stored_keys, (0, 2, 3, 1))
    return (stored_keys, stored_values)


def solution(mesh):
    in_specs = (
        P("ens", ("ctx", "group"), None),
        P("ens", ("ctx", "group"), None),
        P(),
        P("ens", "group", None),
        P("ens", "group", None),
    )
    out_specs = (P(("ens", "ctx"), "group", None, None), P(("ens", "ctx"), None, "group", None))
    return jax.shard_map(
        per_device, mesh=mesh, in_specs=in_specs, out_specs=out_specs, check_vma=False
    )
```

profile of v0, /device:TPU:1, one launch (start us, length us, event | category | flops | bytes accessed | tf_op | source)
XLA Modules:
  0.0 120.7 jit_solution(424359039690574848)
XLA Ops:
  7.2 0.0 copy-start
  7.2 0.0 copy-start.2
  7.2 0.0 all-gather.2.cloned.1.call-start
  7.2 1.3 %fusion.1 = f32[16,32]{1,0:T(8,128)S(1)} fusion(bf16[16,32,512]{2,1,0:T(8,128)(2,1)} %param.5), kind=kLoop, calls=%fused_computation.6 | loop fusion | flops 785920 | bytes 526336 | tf_op jit(solution)/shard_map/reduce_sum | solution.py:35
  8.5 1.2 %fusion.3 = bf16[16,32,512]{2,1,0:T(8,128)(2,1)S(1)} fusion(bf16[16,32,512]{2,1,0:T(8,128)(2,1)} %param.5, f32[512]{0:T(512)} %param.7, f32[16,32]{1,0:T(8,128)S(1)} %add_rsqrt_fusion), kind=kLoop, calls=%fused_computation.8 | loop fusion | flops 1048576 | bytes 1052672 | tf_op jit(solution)/shard_map/convert_element_type | solution.py:40
  9.8 1.0 pad_maximum_fusion
  10.7 19.2 %all_to_all.12 = bf16[16,32,576]{2,1,0:T(8,128)(2,1)S(1)} all-to-all(bf16[16,32,576]{2,1,0:T(8,128)(2,1)S(1)} %pad_maximum_fusion), channel_id=1, replica_groups=mesh['ens'=2,'ctx'=16,'group'=8] {'ctx'}, dimensions={0} | all-to-all | bytes 1179648 | tf_op jit(solution)/shard_map/all_to_all | solution.py:15
  30.0 0.8 split.8
  30.8 0.0 all-gather.2.cloned.1.call-update
  30.8 0.0 copy-done.2
  30.8 0.2 copy.14
  31.0 0.1 copy.15
  31.1 26.3 %all_gather.7 = bf16[1,16,256,64]{3,1,0,2:T(8,128)(2,1)S(1)} all-gather(bf16[1,16,32,64]{3,1,0,2:T(8,128)(2,1)S(1)} %copy.15), channel_id=1, replica_groups=mesh['ens'=2,'ctx'=16,'group'=8] {'group'}, dimensions={2}, use_global_device_ids=true | all-gather | bytes 589824 | tf_op jit(solution)/shard_map/all_gather | solution.py:50
  57.4 1.3 %copy.16 = bf16[1,16,256,64]{2,1,3,0:T(8,128)(2,1)S(1)} copy(bf16[1,16,256,64]{3,1,0,2:T(8,128)(2,1)S(1)} %all_gather.7) | data formatting | bytes 1048576 | tf_op jit(solution)/shard_map/all_gather | solution.py:50
  58.7 0.2 copy.19
  58.9 28.0 %all-gather.2.cloned.1.call-done = bf16[1,16,256,512]{3,2,1,0:T(8,128)(2,1)} async-done(((bf16[1,16,32,512]{3,2,1,0:T(8,128)(2,1)}), bf16[1,16,256,512]{3,2,1,0:T(8,128)(2,1)}) %all-gather.2.cloned.1.call-update) | async-done | bytes 4194320 | tf_op jit(solution)/shard_map/all_gather | solution.py:49
  86.8 3.5 %fusion.5 = f32[4096,256]{0,1:S(1)} fusion(bf16[4096,512]{1,0:T(8,128)(2,1)} %bitcast.23, bf16[512,256]{0,1:T(8,128)(2,1)S(1)} %bitcast.30), kind=kOutput, calls=%fused_computation.12 | convolution fusion | flops 1073741824 | bytes 8650752
  90.3 0.3 convert_bitcast_fusion
  90.6 0.0 copy-done
  90.6 1.9 %copy-done.1 = bf16[1,16,256,512]{3,2,1,0:T(8,128)(2,1)S(1)} copy-done((bf16[1,16,256,512]{3,2,1,0:T(8,128)(2,1)S(1)}, bf16[1,16,256,512]{3,2,1,0:T(8,128)(2,1)}, u32[]{:S(2)}) %copy-start.1) | copy-done | bytes 4194328
  92.5 1.3 %fusion = bf16[1,4096,2,128]{3,1,2,0:T(8,128)(2,1)S(1)} fusion(bf16[4096,512,1]{1,0,2:T(8,128)(2,1)S(1)} %bitcast.24, bf16[512,2,128]{2,1,0:T(2,128)(2,1)S(1)} %copy-done), kind=kOutput, calls=%fused_computation.1 | convolution fusion | flops 1074790400 | bytes 6553600 | tf_op jit(solution)/shard_map/btr,rhk->bthk/dot_general | solution.py:27
  93.8 18.1 %copy.18 = bf16[1,4096,2,128]{3,2,1,0:T(2,128)(2,1)} copy(bf16[1,4096,2,128]{3,1,2,0:T(8,128)(2,1)S(1)} %fusion) | data formatting | bytes 4194304
  111.9 0.1 broadcast_in_dim.10
  112.0 1.9 %maximum_bitcast_fusion = bf16[1,2,192,4096]{3,2,1,0:T(8,128)(2,1)} fusion(bf16[1,4096,2,64]{1,3,2,0:T(8,128)(2,1)S(1)} %broadcast_in_dim.10, bf16[1,4096,2,128]{1,3,2,0:T(8,128)(2,1)S(1)} %convert_bitcast_fusion), kind=kLoop, calls=%fused_computation.2 | loop fusion | flops 6291456 | bytes 6291456 | tf_op jit(solution)/shard_map/transpose | solution.py:55
  (3 shorter events, 0.0 us)
Async XLA Ops:
  7.2 83.5 %copy-start = (bf16[512,2,128]{2,1,0:T(2,128)(2,1)S(1)}, bf16[512,2,128]{2,1,0:T(2,128)(2,1)}, u32[]{:S(2)}) copy-start(bf16[512,2,128]{2,1,0:T(2,128)(2,1)} %param.9) | copy-start | bytes 786436
  7.2 23.7 %copy-start.2 = (bf16[512,2,128]{2,1,0:T(2,128)(2,1)S(1)}, bf16[512,2,128]{2,1,0:T(2,128)(2,1)}, u32[]{:S(2)}) copy-start(bf16[512,2,128]{2,1,0:T(2,128)(2,1)} %param.8) | copy-start | bytes 786436
  7.2 79.7 %all-gather.2.cloned.1.call-start = ((), (), s32[]{:S(2)}) async-start(), calls=%async_computation.1 | async-start | bytes 4718592 | tf_op jit(solution)/shard_map/all_gather | solution.py:49
  90.3 2.2 %copy-start.1 = (bf16[1,16,256,512]{3,2,1,0:T(8,128)(2,1)S(1)}, bf16[1,16,256,512]{3,2,1,0:T(8,128)(2,1)}, u32[]{:S(2)}) copy-start(bf16[1,16,256,512]{3,2,1,0:T(8,128)(2,1)} %all-gather.2.cloned.1.call-done) | copy-start | bytes 12582916
Sparse Core Ops, SparseCore 0:
  31.0 55.8 all-gather.1
where the time goes:
time: 121 us
  blocking collectives  45.5 us (38%)
  waiting for transfers between devices  28 us (23%)
  local copies, waits for them, and re-layouts  22.7 us (19%)
  between operations  14.2 us (12%)
  other arithmetic  5.63 us (5%)
  matrix products  4.72 us (4%)
    all_gather x1, waiting for transfers between devices, per_device(): lax.all_gather(rows_cut, 'group', axis=2, tiled=True)  28 us
    all_gather x1, blocking collectives, per_device(): lax.all_gather(rotary_cut, 'group', axis=2, tiled=True)  26.3 us
    unnamed x9, local copies, waits for them, and re-layouts  20.4 us
    all_to_all x1, blocking collectives, in_one_piece(): lax.all_to_all(both, axis, split_axis=split_dim, concat_axis=concat_dim,...  19.2 us
    unnamed x1, matrix products  3.47 us
  transfers between devices with their start and end apart: 1, of which 1 were waited for; matrix products, arithmetic and copies ran while one was open for 1% of the time, Pallas kernels for 0%

commit v1 on v0

v1 whole, which is shorter than its diff:
```python
import jax
import jax.numpy as jnp
from jax import lax
from jax.experimental import pallas as pl
from jax.experimental.pallas import tpu as pltpu
from jax.sharding import PartitionSpec as P

MESH = pl.DeviceIdType.MESH
F32 = jnp.float32
BF16 = jnp.bfloat16
LAG_B, LAG_C, LAG_D = 3, 7, 8
ROT_SEND, ROT_PASS, ROT_PAIR, ROT_DONE = 6, 9, 13, 15


def gray(i):
    return i + i // 2 - 2 * (i // 3)


def kernel(lat, rot, gain, kup, vup, keys_out, vals_out,
           latv, rows, stage, rotv, rxb, ryb, rrows, kraw, vraw, gainv, wtmp, kt, vw, vtmp,
           loc_sem, xs_send, xs_recv, xy_recv, y_send,
           z1_send, z1_recv, z2_send, z2_recv, d_send, d_recv,
           rx_send, rx_recv, ry_send, ry_recv,
           rz_send, rz_recv, rd_send, rd_recv):
    e, c, g = lax.axis_index("ens"), lax.axis_index("ctx"), lax.axis_index("group")
    x, y = c % 4, c // 4
    partner = g + 1 - 2 * (g % 2)

    def at_xy(xx, yy):
        return (e, yy * 4 + xx, g)

    def at_group(gg):
        return (e, c, gg)

    def remote(src, dst, send, recv, dev):
        return pltpu.make_async_remote_copy(
            src_ref=src, dst_ref=dst, send_sem=send, recv_sem=recv,
            device_id=dev, device_id_type=MESH)

    barrier = pltpu.get_barrier_semaphore()
    for i in range(1, 4):
        pl.semaphore_signal(barrier, inc=1, device_id=at_xy((x + i) % 4, y), device_id_type=MESH)
        pl.semaphore_signal(barrier, inc=1, device_id=at_xy(x, (y + i) % 4), device_id_type=MESH)
    for gg in ((g + 2) % 8, (g + 6) % 8, partner):
        pl.semaphore_signal(barrier, inc=1, device_id=at_group(gg), device_id_type=MESH)

    local = [
        pltpu.make_async_copy(lat.at[c], rows.at[c, g], loc_sem.at[0]),
        pltpu.make_async_copy(lat, latv, loc_sem.at[1]),
        pltpu.make_async_copy(rot, rotv, loc_sem.at[2]),
        pltpu.make_async_copy(kup, kraw, loc_sem.at[3]),
        pltpu.make_async_copy(vup, vraw, loc_sem.at[4]),
        pltpu.make_async_copy(gain, gainv, loc_sem.at[5]),
    ]
    for copy in local:
        copy.start()
    local[0].wait()
    local[1].wait()
    pl.semaphore_wait(barrier, 9)

    def column_of(t):
        return ((y + gray(t // 4)) % 4) * 4 + (x + gray(t % 4)) % 4

    def z1(t, way):
        k = column_of(t)
        block = rows.at[k, g]
        return remote(block, block, z1_send.at[way, t], z1_recv.at[way, t],
                      at_group((g + 2 + 4 * way) % 8))

    def z1_wait(t, way):
        k = column_of(t)
        block = rows.at[k, (g + 6 + 4 * way) % 8]
        remote(block, block, z1_send.at[way, t], z1_recv.at[way, t], at_group(g)).wait_recv()

    def z2(t):
        k = column_of(t)
        way = t % 2
        block = rows.at[k, (g + 6 + 4 * way) % 8]
        return remote(block, block, z2_send.at[t], z2_recv.at[t],
                      at_group((g + 2 + 4 * way) % 8))

    def z2_wait(t):
        k = column_of(t)
        block = rows.at[k, (g + 4) % 8]
        remote(block, block, z2_send.at[t], z2_recv.at[t], at_group(g)).wait_recv()

    def push(t, hop):
        block = rows.at[column_of(t), (g + 2 * hop) % 8]
        return remote(block, block, d_send.at[hop, t], d_recv.at[hop, t], at_group(partner))

    def pushed(t, hop):
        block = rows.at[column_of(t), (partner + 2 * hop) % 8]
        remote(block, block, d_send.at[hop, t], d_recv.at[hop, t], at_group(g)).wait_recv()

    def x_direct(i):
        to = (x + 4 - gray(i)) % 4
        return remote(latv.at[y * 4 + to], rows.at[c, g], xs_send.at[i, 0], xy_recv.at[i],
                      at_xy(to, y))

    def x_stage(i, j):
        to = (x + 4 - gray(i)) % 4
        last = (y + 4 - gray(j)) % 4
        return remote(latv.at[last * 4 + to], stage.at[j - 1, i], xs_send.at[i, j],
                      xs_recv.at[i, j], at_xy(to, y))

    def y_send_of(i, j):
        to = (y + 4 - gray(j)) % 4
        if i == 0:
            src = latv.at[to * 4 + x]
        else:
            src = stage.at[j - 1, i]
        return remote(src, rows.at[y * 4 + (x + gray(i)) % 4, g], y_send.at[i, j],
                      xy_recv.at[4 * j + i], at_xy(x, to))

    def arrived(t):
        block = rows.at[column_of(t), g]
        remote(block, block, y_send.at[0, 0], xy_recv.at[t], at_xy(x, y)).wait_recv()

    def rx(i):
        to = (x + 4 - gray(i)) % 4
        return remote(rotv.at[:, to], rxb.at[x], rx_send.at[i], rx_recv.at[i], at_xy(to, y))

    def rx_wait(i):
        remote(rxb.at[0], rxb.at[(x + gray(i)) % 4], rx_send.at[i], rx_recv.at[i],
               at_xy(x, y)).wait_recv()

    def ry(j):
        to = (y + 4 - gray(j)) % 4
        return remote(rxb.at[:, to], ryb.at[y], ry_send.at[j], ry_recv.at[j], at_xy(x, to))

    def ry_wait(j):
        remote(ryb.at[0], ryb.at[(y + gray(j)) % 4], ry_send.at[j], ry_recv.at[j],
               at_xy(x, y)).wait_recv()

    def rz1(way):
        return remote(rrows.at[g], rrows.at[g], rz_send.at[way], rz_recv.at[way],
                      at_group((g + 2 + 4 * way) % 8))

    def rz1_wait(way):
        block = rrows.at[(g + 6 + 4 * way) % 8]
        remote(block, block, rz_send.at[way], rz_recv.at[way], at_group(g)).wait_recv()

    def rz2(way):
        block = rrows.at[(g + 6 + 4 * way) % 8, pl.ds(4 * way, 4)]
        return remote(block, block, rz_send.at[2 + way], rz_recv.at[2 + way],
                      at_group((g + 2 + 4 * way) % 8))

    def rz2_wait(way):
        block = rrows.at[(g + 4) % 8, pl.ds(4 * way, 4)]
        remote(block, block, rz_send.at[2 + way], rz_recv.at[2 + way], at_group(g)).wait_recv()

    def rpush(hop):
        block = rrows.at[(g + 2 * hop) % 8]
        return remote(block, block, rd_send.at[hop], rd_recv.at[hop], at_group(partner))

    def rpushed(hop):
        block = rrows.at[(partner + 2 * hop) % 8]
        remote(block, block, rd_send.at[hop], rd_recv.at[hop], at_group(g)).wait_recv()

    for way in range(2):
        z1(0, way).start()
    for i in range(1, 4):
        x_direct(i).start()
    for j in range(1, 4):
        y_send_of(0, j).start()
    for j in range(1, 4):
        for i in range(1, 4):
            x_stage(i, j).start()
    push(0, 0).start()
    local[2].wait()
    for i in range(1, 4):
        rx(i).start()
    rxb[pl.ds(x, 1)] = rotv[:, pl.ds(x, 1)].reshape(1, 4, 32, 64)

    @pl.loop(1, 16 + LAG_D)
    def _(t):
        @pl.when(t < 16)
        def _():
            arrived(t)
            for way in range(2):
                z1(t, way).start()
            push(t, 0).start()

        @pl.when(t == 3)
        def _():
            for j in range(1, 4):
                for i in range(1, 4):
                    block = stage.at[j - 1, i]
                    remote(block, block, xs_send.at[i, j], xs_recv.at[i, j],
                           at_xy(x, y)).wait_recv()
                    y_send_of(i, j).start()
            for i in range(1, 4):
                rx_wait(i)
            for j in range(1, 4):
                ry(j).start()
            ryb[pl.ds(y, 1)] = rxb[:, pl.ds(y, 1)].reshape(1, 4, 32, 64)

        @pl.when(t == 4)
        def _():
            for copy in local[3:]:
                copy.wait()
            wtmp[...] = kraw[...].astype(F32)
            for h in range(2):
                kt[pl.ds(h * 128, 128), :] = wtmp[pl.ds(h, 512, 2), :].T.astype(BF16)
            wtmp[...] = vraw[...].astype(F32)
            for h in range(2):
                vw[:, pl.ds(h * 128, 128)] = wtmp[pl.ds(h, 512, 2), :].astype(BF16)

        @pl.when(t == ROT_SEND - 1)
        def _():
            for j in range(1, 4):
                ry_wait(j)
            low, high = ryb[0:2], ryb[2:4]
            rrows[pl.ds(g, 1)] = jnp.concatenate([low, high], axis=-1).reshape(1, 8, 32, 128)

        @pl.when(t == ROT_SEND)
        def _():
            for way in range(2):
                rz1(way).start()
            rpush(0).start()

        @pl.when((t >= LAG_B) & (t < 16 + LAG_B))
        def _():
            u = t - LAG_B
            for way in range(2):
                z1_wait(u, way)
            z2(u).start()
            push(u, 3).start()
            push(u, 1).start()

        @pl.when(t == ROT_PASS)
        def _():
            for way in range(2):
                rz1_wait(way)
            for way in range(2):
                rz2(way).start()
            rpush(3).start()
            rpush(1).start()

        @pl.when(t == ROT_PAIR)
        def _():
            for way in range(2):
                rz2_wait(way)
            rpush(2).start()

        @pl.when((t >= LAG_C) & (t < 16 + LAG_C))
        def _():
            u = t - LAG_C
            z2_wait(u)
            push(u, 2).start()

        @pl.when(t >= LAG_D)
        def _():
            u = t - LAG_D
            for hop in range(4):
                pushed(u, hop)
            k = column_of(u)
            one = rows[pl.ds(k, 1)].reshape(256, 512).astype(F32)
            mean = jnp.mean(one * one, axis=-1, keepdims=True)
            ready = (one * lax.rsqrt(mean + 1e-06) * gainv[...]).astype(BF16)
            wide = lax.dot_general(kt[...], ready, (((1,), (1,)), ((), ())),
                                   preferred_element_type=F32)
            at = pl.ds(pl.multiple_of(k * 256, 256), 256)
            for h in range(2):
                keys_out[h, pl.ds(0, 128), at] = wide[h * 128:(h + 1) * 128].astype(BF16)
            vals = jnp.dot(ready, vw[...], preferred_element_type=F32)
            for h in range(2):
                vtmp[pl.ds(h, 256, 2), :] = vals[:, h * 128:(h + 1) * 128]
            vals_out[pl.ds(pl.multiple_of(k * 512, 512), 512), :] = vtmp[...].astype(BF16)

        @pl.when(t == ROT_DONE)
        def _():
            for hop in range(4):
                rpushed(hop)

            @pl.loop(0, 8)
            def _(n):
                pair = rrows[:, pl.ds(n, 1)].reshape(256, 128).astype(F32).T.astype(BF16)
                for half in range(2):
                    at = pl.ds(pl.multiple_of((n + 8 * half) * 256, 256), 256)
                    for h in range(2):
                        keys_out[h, pl.ds(128, 64), at] = pair[half * 64:(half + 1) * 64]

    for i in range(1, 4):
        for j in range(4):
            block = stage.at[0, 0]
            remote(block, block, xs_send.at[i, j], xy_recv.at[0], at_xy(x, y)).wait_send()
    for i in range(4):
        for j in range(1, 4):
            block = stage.at[0, 0]
            remote(block, block, y_send.at[i, j], xy_recv.at[0], at_xy(x, y)).wait_send()
    for i in range(1, 4):
        rx(i).wait_send()
        ry(i).wait_send()
    for way in range(2):
        rz1(way).wait_send()
        rz2(way).wait_send()
    for hop in range(4):
        rpush(hop).wait_send()

    @pl.loop(0, 16)
    def _(t):
        for way in range(2):
            z1(t, way).wait_send()
        z2(t).wait_send()
        for hop in range(4):
            push(t, hop).wait_send()


def per_device(latents, rotary_rows, latent_gain, key_up, value_up):
    dma = pltpu.SemaphoreType.DMA
    any_spec = pl.BlockSpec(memory_space=pltpu.HBM)
    keys, vals = pl.pallas_call(
        kernel,
        out_shape=(
            jax.ShapeDtypeStruct((2, 192, 4096), BF16),
            jax.ShapeDtypeStruct((8192, 128), BF16),
        ),
        in_specs=[any_spec] * 5,
        out_specs=[pl.BlockSpec(memory_space=pltpu.VMEM)] * 2,
        scratch_shapes=[
            pltpu.VMEM((16, 32, 512), BF16),
            pltpu.VMEM((16, 8, 32, 512), BF16),
            pltpu.VMEM((3, 4, 32, 512), BF16),
            pltpu.VMEM((4, 4, 32, 64), BF16),
            pltpu.VMEM((4, 4, 32, 64), BF16),
            pltpu.VMEM((4, 4, 32, 64), BF16),
            pltpu.VMEM((8, 8, 32, 128), BF16),
            pltpu.VMEM((1024, 128), BF16),
            pltpu.VMEM((1024, 128), BF16),
            pltpu.VMEM((1, 512), F32),
            pltpu.VMEM((1024, 128), F32),
            pltpu.VMEM((256, 512), BF16),
            pltpu.VMEM((512, 256), BF16),
            pltpu.VMEM((512, 128), F32),
            dma((7,)),
            dma((4, 4)), dma((4, 4)), dma((16,)), dma((4, 4)),
            dma((2, 16)), dma((2, 16)), dma((16,)), dma((16,)), dma((4, 16)), dma((4, 16)),
            dma((4,)), dma((4,)), dma((4,)), dma((4,)),
            dma((4,)), dma((4,)), dma((4,)), dma((4,)),
        ],
        compiler_params=pltpu.CompilerParams(
            collective_id=0, has_side_effects=True, vmem_limit_bytes=40 * 1024 * 1024),
        name="expand",
    )(*(pltpu.with_memory_space_constraint(a, pltpu.HBM) for a in (
        latents, rotary_rows.reshape(4, 4, 32, 64), latent_gain.reshape(1, 512),
        key_up.reshape(1024, 128), value_up.reshape(1024, 128))))
    return keys.reshape(1, 2, 192, 4096), vals.reshape(1, 4096, 2, 128)


def solution(mesh):
    in_specs = (
        P("ens", ("ctx", "group"), None),
        P("ens", ("ctx", "group"), None),
        P(),
        P("ens", "group", None),
        P("ens", "group", None),
    )
    out_specs = (P(("ens", "ctx"), "group", None, None), P(("ens", "ctx"), None, "group", None))
    return jax.shard_map(
        per_device, mesh=mesh, in_specs=in_specs, out_specs=out_specs, check_vma=False
    )
```

time: 121 us -> 64.4 us (0.53)
  Pallas kernels: 0 us -> 60.7 us
  blocking collectives: 45.5 us -> 0 us
  waiting for transfers between devices: 28 us -> 0 us
  local copies, waits for them, and re-layouts: 22.7 us -> 2.99 us
  between operations: 14.2 us -> 0.64 us
  other arithmetic: 5.63 us -> 0 us
  matrix products: 4.72 us -> 0 us
    pallas_call x0 -> x1, Pallas kernels: none -> 60.7 us  [per_device(): pl.pallas_call(kernel, out_shape=(jax.ShapeDtypeStruct((2, 192, 4096), BF...]
    all_gather x1 -> x0, waiting for transfers between devices: 28 us -> none  [per_device(): lax.all_gather(rows_cut, 'group', axis=2, tiled=True)]
    all_gather x1 -> x0, blocking collectives: 26.3 us -> none  [per_device(): lax.all_gather(rotary_cut, 'group', axis=2, tiled=True)]
    all_to_all x1 -> x0, blocking collectives: 19.2 us -> none  [in_one_piece(): lax.all_to_all(both, axis, split_axis=split_dim, concat_axis=concat_dim,...]
    unnamed x9 -> x2, local copies, waits for them, and re-layouts: 20.4 us -> 2.99 us
    unnamed x1 -> x0, matrix products: 3.47 us -> none
    transpose x1 -> x0, other arithmetic: 1.87 us -> none  [per_device(): stored_keys = jnp.transpose(stored_keys, (0, 2, 3, 1))]
    convert_element_type x2 -> x0, other arithmetic: 1.51 us -> none  [the longest x1 1.23 us: per_device(): root_norm(latents.astype(jnp.float32), latent_gain).astype(jnp.bfloat16)]
  transfers between devices with their start and end apart: 1 -> 0, of which waited for: 1 -> 0; matrix products, arithmetic and copies ran while one was open for 1% -> 0% of each run, Pallas kernels for 0% -> 0%
where the time goes in v1:
time: 64.4 us; the launch traced here: 64.3 us
  Pallas kernels  60.7 us (94%)
  local copies, waits for them, and re-layouts  2.99 us (5%)
    pallas_call x1, Pallas kernels, per_device(): pl.pallas_call(kernel, out_shape=(jax.ShapeDtypeStruct((2, 192, 4096), BF...  60.7 us
    unnamed x2, local copies, waits for them, and re-layouts  2.99 us

profile of v1, /device:TPU:1, one launch (start us, length us, event | category | flops | bytes accessed | tf_op | source)
XLA Modules:
  0.0 64.3 jit_solution(5472827462121119134)
XLA Ops:
  0.6 60.7 %expand.1 = (bf16[2,192,4096]{2,1,0:T(8,128)(2,1)S(1)}, bf16[8192,128]{1,0:T(8,128)(2,1)S(1)}) custom-call(bf16[16,32,512]{2,1,0:T(8,128)(2,1)} %lat.1, bf16[4,4,32,64]{3,2,1,0:T(8,128)(2,1)} %bitcast.10, f32[1,512]{1,0:T(1,128)} %bitcast.11, bf16[1024,128]{1,0:T(8,128)(2,1)} %bitcast.8, bf16[1024,128]{1,0:T(8,128)(2,1)} %bitcast.9), custom_call_target="tpu_custom_call" | custom-call | tf_op jit(solution)/shard_map/expand/pallas_call | solution.py:313
  61.3 1.7 %copy.9 = bf16[1,2,192,4096]{3,2,1,0:T(8,128)(2,1)} copy(bf16[1,2,192,4096]{3,2,1,0:T(8,128)(2,1)S(1)} %bitcast.6) | data formatting | bytes 6291456
  63.0 1.3 %copy.10 = bf16[1,4096,2,128]{3,2,1,0:T(2,128)(2,1)} copy(bf16[1,4096,2,128]{3,2,1,0:T(2,128)(2,1)S(1)} %bitcast.7) | data formatting | bytes 4194304

commit v2 on v1

v2 whole, which is shorter than its diff:
```python
import jax
import jax.numpy as jnp
from jax import lax
from jax.experimental import pallas as pl
from jax.experimental.pallas import tpu as pltpu
from jax.sharding import PartitionSpec as P

MESH = pl.DeviceIdType.MESH
F32 = jnp.float32
BF16 = jnp.bfloat16
LAG_B, LAG_C, LAG_D = 3, 7, 8
ROT_Z, ROT_X, ROT_Y, ROT_PUSH, ROT_DONE = 4, 8, 11, 14, 16


def gray(i):
    return i + i // 2 - 2 * (i // 3)


def kernel(lat, rot, gain, kup, vup, keys_out, vals_out,
           latv, rows, stage, rotv, rz, rx, ry, rt, kraw, vraw, gainv, wtmp, kt, vw, vtmp,
           loc_sem, x_send, y_send, z_send, d_send, r_send,
           xs_recv, xy_recv, z1_recv, z2_recv, d_recv,
           rz1_recv, rz2_recv, rx_recv, ry_recv, rd_recv):
    e, c, g = lax.axis_index("ens"), lax.axis_index("ctx"), lax.axis_index("group")
    x, y = c % 4, c // 4
    zh, core = g // 2, g % 2
    partner = g + 1 - 2 * core

    def at_xy(xx, yy):
        return (e, yy * 4 + xx, g)

    def at_group(gg):
        return (e, c, gg)

    def remote(src, dst, send, recv, dev):
        return pltpu.make_async_remote_copy(
            src_ref=src, dst_ref=dst, send_sem=send, recv_sem=recv,
            device_id=dev, device_id_type=MESH)

    def got(block, recv):
        remote(block, block, x_send, recv, at_group(g)).wait_recv()

    def sent(block, send):
        remote(block, block, send, xy_recv.at[0], at_group(g)).wait_send()

    barrier = pltpu.get_barrier_semaphore()
    for i in range(1, 4):
        pl.semaphore_signal(barrier, inc=1, device_id=at_xy((x + i) % 4, y), device_id_type=MESH)
        pl.semaphore_signal(barrier, inc=1, device_id=at_xy(x, (y + i) % 4), device_id_type=MESH)
    for gg in ((g + 2) % 8, (g + 6) % 8, partner):
        pl.semaphore_signal(barrier, inc=1, device_id=at_group(gg), device_id_type=MESH)

    local = [
        pltpu.make_async_copy(rot, rotv, loc_sem.at[0]),
        pltpu.make_async_copy(lat.at[c], rows.at[c, g], loc_sem.at[1]),
        pltpu.make_async_copy(lat, latv, loc_sem.at[2]),
        pltpu.make_async_copy(kup, kraw, loc_sem.at[3]),
        pltpu.make_async_copy(vup, vraw, loc_sem.at[4]),
        pltpu.make_async_copy(gain, gainv, loc_sem.at[5]),
    ]
    for copy in local:
        copy.start()
    local[0].wait()
    rz[pl.ds(zh, 1)] = jnp.concatenate([rotv[0:2], rotv[2:4]], axis=-1).reshape(1, 2, 4, 32, 128)
    local[1].wait()
    local[2].wait()
    pl.semaphore_wait(barrier, 9)

    def column_of(t):
        far, both = (t + 12) // 16, (t + 9) // 16
        i = (1 - far) * t + both * (1 + (t + 2) % 3)
        j = far * (1 - both) * (t - 3) + both * ((t + 2) // 3 - 2)
        return ((y + gray(j)) % 4) * 4 + (x + gray(i)) % 4

    def order(i, j):
        return i if j == 0 else 3 + j if i == 0 else 3 + 3 * j + i

    def along(way):
        return at_group((g + 2 + 4 * way) % 8)

    def z1(t, way):
        block = rows.at[column_of(t), g]
        return remote(block, block, z_send, z1_recv.at[t], along(way))

    def z2(t):
        way = t % 2
        block = rows.at[column_of(t), (g + 6 + 4 * way) % 8]
        return remote(block, block, z_send, z2_recv.at[t], along(way))

    def push(t, hop):
        block = rows.at[column_of(t), (g + 2 * hop) % 8]
        return remote(block, block, d_send, d_recv.at[t], at_group(partner))

    def x_direct(i):
        to = (x + 4 - gray(i)) % 4
        return remote(latv.at[y * 4 + to], rows.at[c, g], x_send, xy_recv.at[i], at_xy(to, y))

    def x_stage(i, j):
        to = (x + 4 - gray(i)) % 4
        last = (y + 4 - gray(j)) % 4
        return remote(latv.at[last * 4 + to], stage.at[j - 1, i - 1], x_send,
                      xs_recv.at[i, j], at_xy(to, y))

    def y_on(i, j):
        to = (y + 4 - gray(j)) % 4
        src = latv.at[to * 4 + x] if i == 0 else stage.at[j - 1, i - 1]
        return remote(src, rows.at[y * 4 + (x + gray(i)) % 4, g], y_send,
                      xy_recv.at[order(i, j)], at_xy(x, to))

    def rz1(way):
        return remote(rz.at[zh], rz.at[zh], r_send.at[0], rz1_recv.at[way], along(way))

    def rz2(way):
        block = rz.at[(zh + 3 + 2 * way) % 4, way]
        return remote(block, block, r_send.at[0], rz2_recv.at[way], along(way))

    def rx_to(i):
        to = (x + 4 - gray(i)) % 4
        return remote(rz.at[:, :, to], rx.at[x], r_send.at[1], rx_recv.at[i], at_xy(to, y))

    def ry_to(j):
        to = (y + 4 - gray(j)) % 4
        return remote(rx.at[:, :, to % 2], ry.at[y, :, :, core], r_send.at[2], ry_recv.at[j],
                      at_xy(x, to))

    def rpush(j):
        block = ry.at[(y + gray(j)) % 4, :, :, core]
        return remote(block, block, r_send.at[3], rd_recv.at[j], at_group(partner))

    for way in range(2):
        z1(0, way).start()
    for way in range(2):
        rz1(way).start()
    for i in range(1, 4):
        x_direct(i).start()
        y_on(0, i).start()
    push(0, 0).start()

    @pl.loop(1, 16 + LAG_D)
    def _(t):
        @pl.when(t < 16)
        def _():
            got(rows.at[column_of(t), g], xy_recv.at[t])
            for way in range(2):
                z1(t, way).start()
            push(t, 0).start()

        @pl.when(t == 2)
        def _():
            for j in range(1, 4):
                for i in range(1, 4):
                    x_stage(i, j).start()

        for j in range(1, 4):
            @pl.when(t == 3 + j)
            def _(j=j):
                for i in range(1, 4):
                    got(stage.at[j - 1, i - 1], xs_recv.at[i, j])
                    y_on(i, j).start()

        @pl.when(t == 7)
        def _():
            for copy in local[3:]:
                copy.wait()
            wtmp[...] = kraw[...].astype(F32)
            for h in range(2):
                kt[pl.ds(h * 128, 128), :] = wtmp[pl.ds(h, 512, 2), :].T.astype(BF16)
            wtmp[...] = vraw[...].astype(F32)
            for h in range(2):
                vw[:, pl.ds(h * 128, 128)] = wtmp[pl.ds(h, 512, 2), :].astype(BF16)

        @pl.when((t >= LAG_B) & (t < 16 + LAG_B))
        def _():
            u = t - LAG_B
            got(rows.at[column_of(u), pl.ds(0, 2)], z1_recv.at[u])
            z2(u).start()
            push(u, 3).start()
            push(u, 1).start()

        @pl.when(t == ROT_Z)
        def _():
            for way in range(2):
                got(rz.at[0], rz1_recv.at[way])
            for way in range(2):
                rz2(way).start()

        @pl.when(t == ROT_X)
        def _():
            for way in range(2):
                got(rz.at[0, 0], rz2_recv.at[way])
            for i in range(1, 4):
                rx_to(i).start()
            rx[pl.ds(x, 1)] = rz[:, :, pl.ds(x, 1)].reshape(1, 4, 2, 32, 128)

        @pl.when(t == ROT_Y)
        def _():
            for i in range(1, 4):
                got(rx.at[0], rx_recv.at[i])
            for j in range(1, 4):
                ry_to(j).start()
            ry[pl.ds(y, 1), :, :, pl.ds(core, 1)] = rx[:, :, pl.ds(y % 2, 1)].reshape(
                1, 4, 4, 1, 32, 128)

        @pl.when(t == ROT_PUSH)
        def _():
            rpush(0).start()
            for j in range(1, 4):
                got(ry.at[0, :, :, 0], ry_recv.at[j])
                rpush(j).start()

        @pl.when((t >= LAG_C) & (t < 16 + LAG_C))
        def _():
            u = t - LAG_C
            got(rows.at[column_of(u), 0], z2_recv.at[u])
            push(u, 2).start()

        @pl.when(t >= LAG_D)
        def _():
            u = t - LAG_D
            k = column_of(u)
            got(rows.at[k, pl.ds(0, 4)], d_recv.at[u])
            one = rows[pl.ds(k, 1)].reshape(256, 512).astype(F32)
            mean = jnp.mean(one * one, axis=-1, keepdims=True)
            ready = (one * lax.rsqrt(mean + 1e-06) * gainv[...]).astype(BF16)
            wide = lax.dot_general(kt[...], ready, (((1,), (1,)), ((), ())),
                                   preferred_element_type=F32)
            at = pl.ds(pl.multiple_of(k * 256, 256), 256)
            for h in range(2):
                keys_out[h, pl.ds(0, 128), at] = wide[h * 128:(h + 1) * 128].astype(BF16)
            vals = jnp.dot(ready, vw[...], preferred_element_type=F32)
            for h in range(2):
                vtmp[pl.ds(h, 256, 2), :] = vals[:, h * 128:(h + 1) * 128]
            vals_out[pl.ds(pl.multiple_of(k * 512, 512), 512), :] = vtmp[...].astype(BF16)

        @pl.when(t == ROT_DONE)
        def _():
            for j in range(4):
                got(ry.at[0, :, :, 0], rd_recv.at[j])

            @pl.loop(0, 16)
            def _(k):
                one = ry[pl.ds(k // 4, 1), pl.ds(k % 4, 1)].reshape(256, 128)
                rt[...] = one.astype(F32).T
                half = rt[pl.ds(pl.multiple_of(y // 2 * 64, 64), 64), :].astype(BF16)
                at = pl.ds(pl.multiple_of(k * 256, 256), 256)
                for h in range(2):
                    keys_out[h, pl.ds(128, 64), at] = half

    sent(latv.at[pl.ds(0, 12)], x_send)
    sent(latv.at[pl.ds(0, 12)], y_send)
    sent(rows.at[pl.ds(0, 6)], z_send)
    sent(rows.at[pl.ds(0, 8)], d_send)
    sent(rz.at[pl.ds(0, 3)], r_send.at[0])
    sent(rx.at[pl.ds(0, 3)], r_send.at[1])
    sent(ry.at[pl.ds(0, 3), :, :, 0], r_send.at[2])
    sent(ry.at[:, :, :, 0], r_send.at[3])


def per_device(latents, rotary_rows, latent_gain, key_up, value_up):
    dma = pltpu.SemaphoreType.DMA
    in_hbm = pl.BlockSpec(memory_space=pltpu.HBM)
    keys, vals = pl.pallas_call(
        kernel,
        out_shape=(
            jax.ShapeDtypeStruct((2, 192, 4096), BF16),
            jax.ShapeDtypeStruct((8192, 128), BF16),
        ),
        in_specs=[in_hbm] * 5,
        out_specs=[pl.BlockSpec(memory_space=pltpu.VMEM)] * 2,
        scratch_shapes=[
            pltpu.VMEM((16, 32, 512), BF16),
            pltpu.VMEM((16, 8, 32, 512), BF16),
            pltpu.VMEM((3, 3, 32, 512), BF16),
            pltpu.VMEM((4, 4, 32, 64), BF16),
            pltpu.VMEM((4, 2, 4, 32, 128), BF16),
            pltpu.VMEM((4, 4, 2, 32, 128), BF16),
            pltpu.VMEM((4, 4, 4, 2, 32, 128), BF16),
            pltpu.VMEM((128, 256), F32),
            pltpu.VMEM((1024, 128), BF16),
            pltpu.VMEM((1024, 128), BF16),
            pltpu.VMEM((1, 512), F32),
            pltpu.VMEM((1024, 128), F32),
            pltpu.VMEM((256, 512), BF16),
            pltpu.VMEM((512, 256), BF16),
            pltpu.VMEM((512, 128), F32),
            dma((6,)), dma, dma, dma, dma, dma((4,)),
            dma((4, 4)), dma((16,)), dma((16,)), dma((16,)), dma((16,)),
            dma((2,)), dma((2,)), dma((4,)), dma((4,)), dma((4,)),
        ],
        compiler_params=pltpu.CompilerParams(
            collective_id=0, has_side_effects=True, vmem_limit_bytes=40 * 1024 * 1024),
        name="expand",
    )(*(pltpu.with_memory_space_constraint(a, pltpu.HBM) for a in (
        latents, rotary_rows.reshape(4, 4, 32, 64), latent_gain.reshape(1, 512),
        key_up.reshape(1024, 128), value_up.reshape(1024, 128))))
    return keys.reshape(1, 2, 192, 4096), vals.reshape(1, 4096, 2, 128)


def solution(mesh):
    in_specs = (
        P("ens", ("ctx", "group"), None),
        P("ens", ("ctx", "group"), None),
        P(),
        P("ens", "group", None),
        P("ens", "group", None),
    )
    out_specs = (P(("ens", "ctx"), "group", None, None), P(("ens", "ctx"), None, "group", None))
    return jax.shard_map(
        per_device, mesh=mesh, in_specs=in_specs, out_specs=out_specs, check_vma=False
    )
```

time: 64.4 us -> 57.9 us (0.90)
  the two profiles are of different devices: /device:TPU:1 before, /device:TPU:35 now
where the time goes in v2:
time: 57.9 us; the launch traced here: 57.8 us
  Pallas kernels  54.1 us (93%)
  local copies, waits for them, and re-layouts  2.99 us (5%)
  between operations  0.64 us (1%)
    pallas_call x1, Pallas kernels, per_device(): pl.pallas_call(kernel, out_shape=(jax.ShapeDtypeStruct((2, 192, 4096), BF...  54.1 us
    unnamed x2, local copies, waits for them, and re-layouts  2.99 us

profile of v2, /device:TPU:35, one launch (start us, length us, event | category | flops | bytes accessed | tf_op | source)
XLA Modules:
  0.0 57.8 jit_solution(7365558382150165955)
XLA Ops:
  0.6 54.1 %expand.1 = (bf16[2,192,4096]{2,1,0:T(8,128)(2,1)S(1)}, bf16[8192,128]{1,0:T(8,128)(2,1)S(1)}) custom-call(bf16[16,32,512]{2,1,0:T(8,128)(2,1)} %lat.1, bf16[4,4,32,64]{3,2,1,0:T(8,128)(2,1)} %bitcast.10, f32[1,512]{1,0:T(1,128)} %bitcast.11, bf16[1024,128]{1,0:T(8,128)(2,1)} %bitcast.8, bf16[1024,128]{1,0:T(8,128)(2,1)} %bitcast.9), custom_call_target="tpu_custom_call" | custom-call | tf_op jit(solution)/shard_map/expand/pallas_call | solution.py:262
  54.8 1.7 %copy.9 = bf16[1,2,192,4096]{3,2,1,0:T(8,128)(2,1)} copy(bf16[1,2,192,4096]{3,2,1,0:T(8,128)(2,1)S(1)} %bitcast.6) | data formatting | bytes 6291456
  56.5 1.3 %copy.10 = bf16[1,4096,2,128]{3,2,1,0:T(2,128)(2,1)} copy(bf16[1,4096,2,128]{3,2,1,0:T(2,128)(2,1)S(1)} %bitcast.7) | data formatting | bytes 4194304

commit v3 on v2

v3 whole, which is shorter than its diff:
```python
import jax
import jax.numpy as jnp
from jax import lax
from jax.experimental import pallas as pl
from jax.experimental.pallas import tpu as pltpu
from jax.sharding import PartitionSpec as P

MESH = pl.DeviceIdType.MESH
F32 = jnp.float32
BF16 = jnp.bfloat16
LAG_B, LAG_C, LAG_D = 3, 7, 8
ROT_EACH = 4
LAST = 1
ROT_Z, ROT_X, ROT_Y, ROT_PUSH, ROT_DONE = 4, 8, 11, 14, 16


def gray(i):
    return i + i // 2 - 2 * (i // 3)


def column_of(t, x, y):
    far, both = (t + 12) // 16, (t + 9) // 16
    i = (1 - far) * t + both * (1 + (t + 2) % 3)
    j = far * (1 - both) * (t - 3) + both * ((t + 2) // 3 - 2)
    return ((y + gray(j)) % 4) * 4 + (x + gray(i)) % 4


def order(i, j):
    return i if j == 0 else 3 + j if i == 0 else 3 + 3 * j + i


def expand_chunk(k, put, rows, gainv, kt, vw, keys_out, vals_out, vtmp):
    one = rows[pl.ds(k, 1)].reshape(256, 512).astype(F32)
    mean = jnp.mean(one * one, axis=-1, keepdims=True)
    ready = (one * lax.rsqrt(mean + 1e-06) * gainv[...]).astype(BF16)
    wide = lax.dot_general(kt[...], ready, (((1,), (1,)), ((), ())),
                           preferred_element_type=F32)
    at = pl.ds(pl.multiple_of(put * 256, 256), 256)
    for h in range(2):
        keys_out[h, pl.ds(0, 128), at] = wide[h * 128:(h + 1) * 128].astype(BF16)
    vals = jnp.dot(ready, vw[...], preferred_element_type=F32)
    for h in range(2):
        vtmp[pl.ds(h, 256, 2), :] = vals[:, h * 128:(h + 1) * 128]
    vals_out[pl.ds(pl.multiple_of(put * 512, 512), 512), :] = vtmp[...].astype(BF16)


def kernel(lat, rot, gain, kup, vup, keys_out, vals_out, rows, gainv, kt, vw,
           latv, stage, rotv, rz, rx, ry, rt, kraw, vraw, wtmp, vtmp,
           loc_sem, send, d_send, xs_recv, xy_recv, z1_recv, z2_recv, d_recv, r_recv):
    e, c, g = lax.axis_index("ens"), lax.axis_index("ctx"), lax.axis_index("group")
    x, y = c % 4, c // 4
    zh, core = g // 2, g % 2
    partner = g + 1 - 2 * core

    def at_xy(xx, yy):
        return (e, yy * 4 + xx, g)

    def at_group(gg):
        return (e, c, gg)

    def remote(src, dst, send, recv, dev):
        return pltpu.make_async_remote_copy(
            src_ref=src, dst_ref=dst, send_sem=send, recv_sem=recv,
            device_id=dev, device_id_type=MESH)

    def got(block, recv):
        remote(block, block, send, recv, at_group(g)).wait_recv()

    def sent(block, sem):
        remote(block, block, sem, xy_recv.at[0], at_group(g)).wait_send()

    barrier = pltpu.get_barrier_semaphore()
    for i in range(1, 4):
        pl.semaphore_signal(barrier, inc=1, device_id=at_xy((x + i) % 4, y), device_id_type=MESH)
        pl.semaphore_signal(barrier, inc=1, device_id=at_xy(x, (y + i) % 4), device_id_type=MESH)
    for gg in ((g + 2) % 8, (g + 6) % 8, partner):
        pl.semaphore_signal(barrier, inc=1, device_id=at_group(gg), device_id_type=MESH)

    local = [
        pltpu.make_async_copy(rot, rotv, loc_sem.at[0]),
        pltpu.make_async_copy(lat.at[c], rows.at[c, g], loc_sem.at[1]),
        pltpu.make_async_copy(lat, latv, loc_sem.at[2]),
        pltpu.make_async_copy(kup, kraw, loc_sem.at[3]),
        pltpu.make_async_copy(vup, vraw, loc_sem.at[4]),
        pltpu.make_async_copy(gain, gainv, loc_sem.at[5]),
    ]
    for copy in local:
        copy.start()
    local[0].wait()
    rz[pl.ds(zh, 1)] = jnp.concatenate([rotv[0:2], rotv[2:4]], axis=-1).reshape(1, 2, 4, 32, 128)
    local[1].wait()
    local[2].wait()
    pl.semaphore_wait(barrier, 9)

    def along(way):
        return at_group((g + 2 + 4 * way) % 8)

    def z1(t, way):
        block = rows.at[column_of(t, x, y), g]
        return remote(block, block, send, z1_recv.at[t % 8], along(way))

    def z2(t):
        way = t % 2
        block = rows.at[column_of(t, x, y), (g + 6 + 4 * way) % 8]
        return remote(block, block, send, z2_recv.at[t % 8], along(way))

    def push(t, hop):
        block = rows.at[column_of(t, x, y), (g + 2 * hop) % 8]
        return remote(block, block, d_send, d_recv.at[t], at_group(partner))

    def x_direct(i):
        to = (x + 4 - gray(i)) % 4
        return remote(latv.at[y * 4 + to], rows.at[c, g], send, xy_recv.at[i], at_xy(to, y))

    def x_stage(i, j):
        to = (x + 4 - gray(i)) % 4
        last = (y + 4 - gray(j)) % 4
        return remote(latv.at[last * 4 + to], stage.at[j - 1, i - 1], send,
                      xs_recv.at[j - 1], at_xy(to, y))

    def y_on(i, j):
        to = (y + 4 - gray(j)) % 4
        src = latv.at[to * 4 + x] if i == 0 else stage.at[j - 1, i - 1]
        return remote(src, rows.at[y * 4 + (x + gray(i)) % 4, g], send,
                      xy_recv.at[order(i, j) if i * j == 0 else 6 + j], at_xy(x, to))

    def rz1(way):
        return remote(rz.at[zh], rz.at[zh], send, r_recv.at[0], along(way))

    def rz2(way):
        block = rz.at[(zh + 3 + 2 * way) % 4, way]
        return remote(block, block, send, r_recv.at[1], along(way))

    def rx_to(i):
        to = (x + 4 - gray(i)) % 4
        return remote(rz.at[:, :, to], rx.at[x], send, r_recv.at[2], at_xy(to, y))

    def ry_to(j):
        to = (y + 4 - gray(j)) % 4
        return remote(rx.at[:, :, to % 2], ry.at[y, :, :, core], send, r_recv.at[3],
                      at_xy(x, to))

    def rpush(j):
        block = ry.at[(y + gray(j)) % 4, :, :, core]
        return remote(block, block, send, r_recv.at[4], at_group(partner))

    for way in range(2):
        z1(0, way).start()
    for way in range(2):
        rz1(way).start()
    for i in range(1, 4):
        x_direct(i).start()
        y_on(0, i).start()
    push(0, 0).start()

    @pl.loop(1, 16 + LAG_D)
    def _(t):
        @pl.when(t < 16)
        def _():
            @pl.when(t < 7)
            def _():
                got(rows.at[column_of(t, x, y), g], xy_recv.at[t])

            for j in range(1, 4):
                @pl.when(t == 4 + 3 * j)
                def _(j=j):
                    got(latv.at[pl.ds(0, 3)], xy_recv.at[6 + j])

            for way in range(2):
                z1(t, way).start()
            push(t, 0).start()

        @pl.when(t == 2)
        def _():
            for j in range(1, 4):
                for i in range(1, 4):
                    x_stage(i, j).start()

        for j in range(1, 4):
            @pl.when(t == 3 + j)
            def _(j=j):
                got(stage.at[j - 1], xs_recv.at[j - 1])
                for i in range(1, 4):
                    y_on(i, j).start()

        @pl.when(t == 7)
        def _():
            for copy in local[3:]:
                copy.wait()
            wtmp[...] = kraw[...].astype(F32)
            for h in range(2):
                kt[pl.ds(h * 128, 128), :] = wtmp[pl.ds(h, 512, 2), :].T.astype(BF16)
            wtmp[...] = vraw[...].astype(F32)
            for h in range(2):
                vw[:, pl.ds(h * 128, 128)] = wtmp[pl.ds(h, 512, 2), :].astype(BF16)

        @pl.when((t >= LAG_B) & (t < 16 + LAG_B))
        def _():
            u = t - LAG_B
            got(rows.at[column_of(u, x, y), pl.ds(0, 2)], z1_recv.at[u % 8])
            z2(u).start()
            push(u, 3).start()
            push(u, 1).start()

        @pl.when(t == ROT_Z)
        def _():
            got(rz.at[pl.ds(0, 2)], r_recv.at[0])
            for way in range(2):
                rz2(way).start()

        @pl.when(t == ROT_X)
        def _():
            got(rz.at[0], r_recv.at[1])
            for i in range(1, 4):
                rx_to(i).start()
            rx[pl.ds(x, 1)] = rz[:, :, pl.ds(x, 1)].reshape(1, 4, 2, 32, 128)

        @pl.when(t == ROT_Y)
        def _():
            got(rx.at[pl.ds(0, 3)], r_recv.at[2])
            for j in range(1, 4):
                ry_to(j).start()
            ry[pl.ds(y, 1), :, :, pl.ds(core, 1)] = rx[:, :, pl.ds(y % 2, 1)].reshape(
                1, 4, 4, 1, 32, 128)

        @pl.when(t == ROT_PUSH)
        def _():
            got(ry.at[pl.ds(0, 3), :, :, 0], r_recv.at[3])
            for j in range(4):
                rpush(j).start()

        @pl.when((t >= LAG_C) & (t < 16 + LAG_C))
        def _():
            u = t - LAG_C
            got(rows.at[column_of(u, x, y), 0], z2_recv.at[u % 8])
            push(u, 2).start()

        @pl.when(t >= LAG_D)
        def _():
            u = t - LAG_D
            k = column_of(u, x, y)
            got(rows.at[k, pl.ds(0, 4)], d_recv.at[u])

            @pl.when(u < 16 - LAST)
            def _():
                expand_chunk(k, k, rows, gainv, kt, vw, keys_out, vals_out, vtmp)

        @pl.when(t == ROT_DONE)
        def _():
            got(ry.at[:, :, :, 0], r_recv.at[4])

        @pl.when((t >= ROT_DONE) & (t < ROT_DONE + 16 // ROT_EACH))
        def _():
            @pl.loop(0, ROT_EACH)
            def _(n):
                k = (t - ROT_DONE) * ROT_EACH + n
                one = ry[pl.ds(k // 4, 1), pl.ds(k % 4, 1)].reshape(256, 128)
                rt[...] = one.astype(F32).T
                half = rt[pl.ds(pl.multiple_of(y // 2 * 64, 64), 64), :].astype(BF16)
                at = pl.ds(pl.multiple_of(k * 256, 256), 256)
                for h in range(2):
                    keys_out[h, pl.ds(128, 64), at] = half

    sent(rows.at[pl.ds(0, 14)], send)
    sent(rows.at[pl.ds(0, 8)], d_send)


def store(keys_in, vals_in, rows, gainv, kt, vw, keys_out, vals_out, keys_last, vals_last, vtmp,
          keys_sem, vals_sem):
    c = lax.axis_index("ctx")
    x, y = c % 4, c // 4

    def put(k):
        return pl.ds(pl.multiple_of(k * 256, 256), 256), pl.ds(pl.multiple_of(k * 512, 512), 512)

    @pl.loop(0, 16 - LAST)
    def _(t):
        at, to = put(column_of(t, x, y))
        pltpu.make_async_copy(keys_in.at[:, :, at], keys_out.at[:, :, at], keys_sem).start()
        pltpu.make_async_copy(vals_in.at[to], vals_out.at[to], vals_sem).start()

    for n in range(LAST):
        at, to = put(column_of(16 - LAST + n, x, y))
        turned = pl.ds(128, 64)
        pltpu.make_async_copy(keys_in.at[:, turned, at], keys_out.at[:, turned, at],
                              keys_sem).start()

    @pl.loop(0, LAST)
    def _(n):
        k = column_of(16 - LAST + n, x, y)
        expand_chunk(k, n, rows, gainv, kt, vw, keys_last, vals_last, vtmp)

    for n in range(LAST):
        at, to = put(column_of(16 - LAST + n, x, y))
        here, there = put(n)
        pltpu.make_async_copy(keys_last.at[:, :, here], keys_out.at[:, pl.ds(0, 128), at],
                              keys_sem).start()
        pltpu.make_async_copy(vals_last.at[there], vals_out.at[to], vals_sem).start()
    pltpu.make_async_copy(keys_in, keys_out, keys_sem).wait()
    pltpu.make_async_copy(vals_in, vals_out, vals_sem).wait()


def per_device(latents, rotary_rows, latent_gain, key_up, value_up):
    dma = pltpu.SemaphoreType.DMA
    hbm = pl.BlockSpec(memory_space=pltpu.HBM)
    vmem = pl.BlockSpec(memory_space=pltpu.VMEM)
    outs = (
        jax.ShapeDtypeStruct((2, 192, 4096), BF16),
        jax.ShapeDtypeStruct((8192, 128), BF16),
    )
    parts = pl.pallas_call(
        kernel,
        out_shape=outs + (
            jax.ShapeDtypeStruct((16, 8, 32, 512), BF16),
            jax.ShapeDtypeStruct((1, 512), F32),
            jax.ShapeDtypeStruct((256, 512), BF16),
            jax.ShapeDtypeStruct((512, 256), BF16),
        ),
        in_specs=[hbm] * 5,
        out_specs=[vmem] * 6,
        scratch_shapes=[
            pltpu.VMEM((16, 32, 512), BF16),
            pltpu.VMEM((3, 3, 32, 512), BF16),
            pltpu.VMEM((4, 4, 32, 64), BF16),
            pltpu.VMEM((4, 2, 4, 32, 128), BF16),
            pltpu.VMEM((4, 4, 2, 32, 128), BF16),
            pltpu.VMEM((4, 4, 4, 2, 32, 128), BF16),
            pltpu.VMEM((128, 256), F32),
            pltpu.VMEM((1024, 128), BF16),
            pltpu.VMEM((1024, 128), BF16),
            pltpu.VMEM((1024, 128), F32),
            pltpu.VMEM((512, 128), F32),
            dma((6,)), dma, dma, dma((3,)), dma((10,)), dma((8,)), dma((8,)), dma((16,)), dma((5,)),
        ],
        compiler_params=pltpu.CompilerParams(
            collective_id=0, has_side_effects=True, vmem_limit_bytes=32 * 1024 * 1024),
        name="expand",
    )(*(pltpu.with_memory_space_constraint(a, pltpu.HBM) for a in (
        latents, rotary_rows.reshape(4, 4, 32, 64), latent_gain.reshape(1, 512),
        key_up.reshape(1024, 128), value_up.reshape(1024, 128))))
    keys, vals = pl.pallas_call(
        store,
        out_shape=outs,
        in_specs=[vmem] * 6,
        out_specs=[hbm] * 2,
        scratch_shapes=[
            pltpu.VMEM((2, 128, LAST * 256), BF16),
            pltpu.VMEM((LAST * 512, 128), BF16),
            pltpu.VMEM((512, 128), F32),
            dma, dma,
        ],
        compiler_params=pltpu.CompilerParams(vmem_limit_bytes=32 * 1024 * 1024),
        name="store",
    )(*parts)
    return keys.reshape(1, 2, 192, 4096), vals.reshape(1, 4096, 2, 128)


def solution(mesh):
    in_specs = (
        P("ens", ("ctx", "group"), None),
        P("ens", ("ctx", "group"), None),
        P(),
        P("ens", "group", None),
        P("ens", "group", None),
    )
    out_specs = (P(("ens", "ctx"), "group", None, None), P(("ens", "ctx"), None, "group", None))
    return jax.shard_map(
        per_device, mesh=mesh, in_specs=in_specs, out_specs=out_specs, check_vma=False
    )
```

time: 57.9 us -> 55.9 us (0.965)
  local copies, waits for them, and re-layouts: 2.99 us -> 0 us
  Pallas kernels: 54.1 us -> 55.2 us
    unnamed x2 -> x0, local copies, waits for them, and re-layouts: 2.99 us -> none
    pallas_call x1 -> x2, Pallas kernels: 54.1 us -> 55.2 us  [the longest x1 52.8 us: per_device(): pl.pallas_call(kernel, out_shape=outs + (jax.ShapeDtypeStruct((16, 8, 32,...]
where the time goes in v3:
time: 55.9 us; the launch traced here: 55.8 us
  Pallas kernels  55.2 us (99%)
  between operations  0.64 us (1%)
    pallas_call x1, Pallas kernels, per_device(): pl.pallas_call(kernel, out_shape=outs + (jax.ShapeDtypeStruct((16, 8, 32,...  52.8 us
    pallas_call x1, Pallas kernels, per_device(): pl.pallas_call(store, out_shape=outs, in_specs=[vmem] * 6, out_specs=[hbm...  2.38 us

profile of v3, /device:TPU:35, one launch (start us, length us, event | category | flops | bytes accessed | tf_op | source)
XLA Modules:
  0.0 55.8 jit_solution(6431076966231080208)
XLA Ops:
  0.6 52.8 %expand.1 = (bf16[2,192,4096]{2,1,0:T(8,128)(2,1)S(1)}, bf16[8192,128]{1,0:T(8,128)(2,1)S(1)}, bf16[16,8,32,512]{3,2,1,0:T(8,128)(2,1)S(1)}, f32[1,512]{1,0:T(1,...) custom-call(bf16[16,32,512]{2,1,0:T(8,128)(2,1)} %lat.1, bf16[4,4,32,64]{3,2,1,0:T(8,128)(2,1)} %bitcast.8, ...), custom_call_target="tpu_custom_call" | custom-call | tf_op jit(solution)/shard_map/expand/pallas_call | solution.py:311
  53.4 2.4 %store.1 = (bf16[2,192,4096]{2,1,0:T(8,128)(2,1)}, bf16[8192,128]{1,0:T(8,128)(2,1)}) custom-call(bf16[2,192,4096]{2,1,0:T(8,128)(2,1)S(1)} %get-tuple-element.10.keys_in, bf16[8192,128]{1,0:T(8,128)(2,1)S(1)} %get-tuple-element.11.vals_in, bf16[16,8,32,512]{3,2,1,0:T(8,128)(2,1)S(1)} %get-tuple-element.12.rows, f32[1,512]{1,0:T(1,128)S(1)} %get-tuple-element.13.gainv, ...), custom_call_target="tpu_custom_call" | custom-call | tf_op jit(solution)/shard_map/store/pallas_call | solution.py:341

commit v4 on v3

--- a/solution.py
+++ b/solution.py
@@ -9,9 +9,8 @@
 F32 = jnp.float32
 BF16 = jnp.bfloat16
 LAG_B, LAG_C, LAG_D = 3, 7, 8
-ROT_EACH = 4
 LAST = 1
-ROT_Z, ROT_X, ROT_Y, ROT_PUSH, ROT_DONE = 4, 8, 11, 14, 16
+ROT_Z, ROT_X, ROT_Y, ROT_PUSH, ROT_DONE = 4, 8, 11, 15, 17
 
 
 def gray(i):
@@ -45,7 +44,7 @@
 
 
 def kernel(lat, rot, gain, kup, vup, keys_out, vals_out, rows, gainv, kt, vw,
-           latv, stage, rotv, rz, rx, ry, rt, kraw, vraw, wtmp, vtmp,
+           latv, stage, rotv, rz, rx, ry, kraw, vraw, wtmp, vtmp,
            loc_sem, send, d_send, xs_recv, xy_recv, z1_recv, z2_recv, d_recv, r_recv):
     e, c, g = lax.axis_index("ens"), lax.axis_index("ctx"), lax.axis_index("group")
     x, y = c % 4, c // 4
@@ -97,7 +96,7 @@
 
     def z1(t, way):
         block = rows.at[column_of(t, x, y), g]
-        return remote(block, block, send, z1_recv.at[t % 8], along(way))
+        return remote(block, block, send, z1_recv.at[t], along(way))
 
     def z2(t):
         way = t % 2
@@ -152,12 +151,20 @@
         x_direct(i).start()
         y_on(0, i).start()
     push(0, 0).start()
+    for j in range(1, 4):
+        for i in range(1, 4):
+            x_stage(i, j).start()
+
+    def forth(t):
+        for way in range(2):
+            z1(t, way).start()
+        push(t, 0).start()
 
     @pl.loop(1, 16 + LAG_D)
     def _(t):
-        @pl.when(t < 16)
-        def _():
-            @pl.when(t < 7)
+        @pl.when((t < 4) | ((t > 6) & (t < 16)))
+        def _():
+            @pl.when(t < 4)
             def _():
                 got(rows.at[column_of(t, x, y), g], xy_recv.at[t])
 
@@ -166,15 +173,13 @@
                 def _(j=j):
                     got(latv.at[pl.ds(0, 3)], xy_recv.at[6 + j])
 
-            for way in range(2):
-                z1(t, way).start()
-            push(t, 0).start()
-
-        @pl.when(t == 2)
-        def _():
-            for j in range(1, 4):
-                for i in range(1, 4):
-                    x_stage(i, j).start()
+            forth(t)
+
+        @pl.when(t == 4)
+        def _():
+            for u in range(4, 7):
+                got(rows.at[column_of(u, x, y), g], xy_recv.at[u])
+                forth(u)
 
         for j in range(1, 4):
             @pl.when(t == 3 + j)
@@ -197,7 +202,7 @@
         @pl.when((t >= LAG_B) & (t < 16 + LAG_B))
         def _():
             u = t - LAG_B
-            got(rows.at[column_of(u, x, y), pl.ds(0, 2)], z1_recv.at[u % 8])
+            got(rows.at[column_of(u, x, y), pl.ds(0, 2)], z1_recv.at[u])
             z2(u).start()
             push(u, 3).start()
             push(u, 1).start()
@@ -249,17 +254,17 @@
         def _():
             got(ry.at[:, :, :, 0], r_recv.at[4])
 
-        @pl.when((t >= ROT_DONE) & (t < ROT_DONE + 16 // ROT_EACH))
-        def _():
-            @pl.loop(0, ROT_EACH)
-            def _(n):
-                k = (t - ROT_DONE) * ROT_EACH + n
-                one = ry[pl.ds(k // 4, 1), pl.ds(k % 4, 1)].reshape(256, 128)
-                rt[...] = one.astype(F32).T
-                half = rt[pl.ds(pl.multiple_of(y // 2 * 64, 64), 64), :].astype(BF16)
-                at = pl.ds(pl.multiple_of(k * 256, 256), 256)
-                for h in range(2):
-                    keys_out[h, pl.ds(128, 64), at] = half
+        @pl.when((t >= ROT_DONE) & (t < ROT_DONE + 4))
+        def _():
+            lane = lax.broadcasted_iota(jnp.int32, (64, 128), 1)
+            number = lax.broadcasted_iota(jnp.int32, (64, 128), 0)
+            pick = (lane == number + y // 2 * 64).astype(F32).astype(BF16)
+            n = t - ROT_DONE
+            one = ry[pl.ds(n, 1)].reshape(1024, 128)
+            turned = lax.dot_general(pick, one, (((1,), (1,)), ((), ())),
+                                     preferred_element_type=F32).astype(BF16)
+            for h in range(2):
+                keys_out[h, pl.ds(128, 64), pl.ds(pl.multiple_of(n * 1024, 1024), 1024)] = turned
 
     sent(rows.at[pl.ds(0, 14)], send)
     sent(rows.at[pl.ds(0, 8)], d_send)
@@ -325,12 +330,11 @@
             pltpu.VMEM((4, 2, 4, 32, 128), BF16),
             pltpu.VMEM((4, 4, 2, 32, 128), BF16),
             pltpu.VMEM((4, 4, 4, 2, 32, 128), BF16),
-            pltpu.VMEM((128, 256), F32),
             pltpu.VMEM((1024, 128), BF16),
             pltpu.VMEM((1024, 128), BF16),
             pltpu.VMEM((1024, 128), F32),
             pltpu.VMEM((512, 128), F32),
-            dma((6,)), dma, dma, dma((3,)), dma((10,)), dma((8,)), dma((8,)), dma((16,)), dma((5,)),
+            dma((6,)), dma, dma, dma((3,)), dma((10,)), dma((16,)), dma((8,)), dma((16,)), dma((5,)),
         ],
         compiler_params=pltpu.CompilerParams(
             collective_id=0, has_side_effects=True, vmem_limit_bytes=32 * 1024 * 1024),

time: 55.9 us -> 55.2 us (0.987)
  the two profiles are of different devices: /device:TPU:35 before, /device:TPU:1 now
where the time goes in v4:
time: 55.2 us; the launch traced here: 54.5 us
  Pallas kernels  53.9 us (98%)
  between operations  0.64 us (1%)
    pallas_call x1, Pallas kernels, per_device(): pl.pallas_call(kernel, out_shape=outs + (jax.ShapeDtypeStruct((16, 8, 32,...  51.5 us
    pallas_call x1, Pallas kernels, per_device(): pl.pallas_call(store, out_shape=outs, in_specs=[vmem] * 6, out_specs=[hbm...  2.38 us

profile of v4, /device:TPU:1, one launch (start us, length us, event | category | flops | bytes accessed | tf_op | source)
XLA Modules:
  0.0 54.5 jit_solution(17633173004940274232)
XLA Ops:
  0.6 51.5 %expand.1 = (bf16[2,192,4096]{2,1,0:T(8,128)(2,1)S(1)}, bf16[8192,128]{1,0:T(8,128)(2,1)S(1)}, bf16[16,8,32,512]{3,2,1,0:T(8,128)(2,1)S(1)}, f32[1,512]{1,0:T(1,...) custom-call(bf16[16,32,512]{2,1,0:T(8,128)(2,1)} %lat.1, bf16[4,4,32,64]{3,2,1,0:T(8,128)(2,1)} %bitcast.8, ...), custom_call_target="tpu_custom_call" | custom-call | tf_op jit(solution)/shard_map/expand/pallas_call | solution.py:316
  52.2 2.4 %store.1 = (bf16[2,192,4096]{2,1,0:T(8,128)(2,1)}, bf16[8192,128]{1,0:T(8,128)(2,1)}) custom-call(bf16[2,192,4096]{2,1,0:T(8,128)(2,1)S(1)} %get-tuple-element.10.keys_in, bf16[8192,128]{1,0:T(8,128)(2,1)S(1)} %get-tuple-element.11.vals_in, bf16[16,8,32,512]{3,2,1,0:T(8,128)(2,1)S(1)} %get-tuple-element.12.rows, f32[1,512]{1,0:T(1,128)S(1)} %get-tuple-element.13.gainv, ...), custom_call_target="tpu_custom_call" | custom-call | tf_op jit(solution)/shard_map/store/pallas_call | solution.py:345

commit v5 on v4

--- a/solution.py
+++ b/solution.py
@@ -8,8 +8,8 @@
 MESH = pl.DeviceIdType.MESH
 F32 = jnp.float32
 BF16 = jnp.bfloat16
-LAG_B, LAG_C, LAG_D = 3, 7, 8
-LAST = 1
+LAG_B, LAG_C, LAG_D = 4, 8, 9
+LAST = 2
 ROT_Z, ROT_X, ROT_Y, ROT_PUSH, ROT_DONE = 4, 8, 11, 15, 17
 
 
@@ -162,6 +162,12 @@
 
     @pl.loop(1, 16 + LAG_D)
     def _(t):
+        @pl.when((t >= LAG_C) & (t < 16 + LAG_C))
+        def _():
+            u = t - LAG_C
+            got(rows.at[column_of(u, x, y), 0], z2_recv.at[u % 8])
+            push(u, 2).start()
+
         @pl.when((t < 4) | ((t > 6) & (t < 16)))
         def _():
             @pl.when(t < 4)
@@ -199,6 +205,16 @@
             for h in range(2):
                 vw[:, pl.ds(h * 128, 128)] = wtmp[pl.ds(h, 512, 2), :].astype(BF16)
 
+        @pl.when(t >= LAG_D)
+        def _():
+            u = t - LAG_D
+            k = column_of(u, x, y)
+            got(rows.at[k, pl.ds(0, 4)], d_recv.at[u])
+
+            @pl.when(u < 16 - LAST)
+            def _():
+                expand_chunk(k, k, rows, gainv, kt, vw, keys_out, vals_out, vtmp)
+
         @pl.when((t >= LAG_B) & (t < 16 + LAG_B))
         def _():
             u = t - LAG_B
@@ -233,22 +249,6 @@
             got(ry.at[pl.ds(0, 3), :, :, 0], r_recv.at[3])
             for j in range(4):
                 rpush(j).start()
-
-        @pl.when((t >= LAG_C) & (t < 16 + LAG_C))
-        def _():
-            u = t - LAG_C
-            got(rows.at[column_of(u, x, y), 0], z2_recv.at[u % 8])
-            push(u, 2).start()
-
-        @pl.when(t >= LAG_D)
-        def _():
-            u = t - LAG_D
-            k = column_of(u, x, y)
-            got(rows.at[k, pl.ds(0, 4)], d_recv.at[u])
-
-            @pl.when(u < 16 - LAST)
-            def _():
-                expand_chunk(k, k, rows, gainv, kt, vw, keys_out, vals_out, vtmp)
 
         @pl.when(t == ROT_DONE)
         def _():

time: 55.2 us -> 55.3 us (level)
  no operation moved by 1% of the time
where the time goes in v5:
time: 55.3 us; the launch traced here: 54.3 us
  Pallas kernels  53.6 us (97%)
  between operations  0.64 us (1%)
    pallas_call x1, Pallas kernels, per_device(): pl.pallas_call(kernel, out_shape=outs + (jax.ShapeDtypeStruct((16, 8, 32,...  51.1 us
    pallas_call x1, Pallas kernels, per_device(): pl.pallas_call(store, out_shape=outs, in_specs=[vmem] * 6, out_specs=[hbm...  2.5 us

profile of v5, /device:TPU:1, one launch (start us, length us, event | category | flops | bytes accessed | tf_op | source)
XLA Modules:
  0.0 54.3 jit_solution(15271336833310245749)
XLA Ops:
  0.6 51.1 %expand.1 = (bf16[2,192,4096]{2,1,0:T(8,128)(2,1)S(1)}, bf16[8192,128]{1,0:T(8,128)(2,1)S(1)}, bf16[16,8,32,512]{3,2,1,0:T(8,128)(2,1)S(1)}, f32[1,512]{1,0:T(1,...) custom-call(bf16[16,32,512]{2,1,0:T(8,128)(2,1)} %lat.1, bf16[4,4,32,64]{3,2,1,0:T(8,128)(2,1)} %bitcast.8, ...), custom_call_target="tpu_custom_call" | custom-call | tf_op jit(solution)/shard_map/expand/pallas_call | solution.py:316
  51.8 2.5 %store.1 = (bf16[2,192,4096]{2,1,0:T(8,128)(2,1)}, bf16[8192,128]{1,0:T(8,128)(2,1)}) custom-call(bf16[2,192,4096]{2,1,0:T(8,128)(2,1)S(1)} %get-tuple-element.10.keys_in, bf16[8192,128]{1,0:T(8,128)(2,1)S(1)} %get-tuple-element.11.vals_in, bf16[16,8,32,512]{3,2,1,0:T(8,128)(2,1)S(1)} %get-tuple-element.12.rows, f32[1,512]{1,0:T(1,128)S(1)} %get-tuple-element.13.gainv, ...), custom_call_target="tpu_custom_call" | custom-call | tf_op jit(solution)/shard_map/store/pallas_call | solution.py:345
